TPU v7x, 256 devices: a whole 4x4x8 slice. The times are simulated.
256 devices in a mesh: items: 4 (over x), users: 64 (over z, y, core).
Axes of the slice: x: 4, y: 4, z: 8, core: 2. Of those that a mesh axis runs over, the one named last changes fastest.
Arguments:
- capsules: bfloat16 [4096, 8, 128], P('users'), may hold values from -6 to 6
- bank: bfloat16 [262144, 128], P(('items', 'users')), may hold values from -0.5 to 0.5
Outputs:
- relative: float32 [4096, 256], P('users', 'items')
- peak: float32 [4096], P('users')
All inputs are finite; a program needn't handle non-finite values.
Results may differ from a plain program's by a relative error of at most 0.0003.
Values may be sent and summed in bfloat16 or wider, within the bound.
A program may use at most 64 MiB of HBM per device.

v0:
```python
import jax
import jax.numpy as jnp
from jax import lax
from jax.sharding import PartitionSpec as P

BLOCK = 1024


def sent_to_all(value, axis):
    length = lax.axis_size(axis)
    return lax.all_to_all(
        jnp.broadcast_to(value[None], (length, *value.shape)), axis, 0, 0, tiled=True
    )


def of_everyone(value, axis):
    return sent_to_all(value, axis).max(axis=0)


def block_peaks(caps, rows):
    users_here = caps.shape[0]
    flat = caps.reshape(users_here * caps.shape[1], caps.shape[2])
    count = rows.shape[0] // BLOCK
    blocks = rows.reshape(count, BLOCK, rows.shape[1])

    def one_block(item_rows):
        score = lax.dot_general(
            flat, item_rows, (((1,), (1,)), ((), ())), preferred_element_type=jnp.float32
        )
        return jnp.max(score.reshape(users_here, -1), axis=1)

    return lax.map(one_block, blocks).T


def per_device(capsules, bank):
    everyone = lax.all_gather(capsules, "users", axis=0, tiled=True)
    own_block = block_peaks(everyone, bank)
    table = lax.all_to_all(own_block, "users", split_axis=0, concat_axis=1, tiled=True)
    peak = of_everyone(jnp.max(table, axis=1), "items")
    return (table - peak[:, None], peak)


def solution(mesh):
    return jax.shard_map(
        per_device,
        mesh=mesh,
        in_specs=(P("users", None, None), P(("items", "users"), None)),
        out_specs=(P("users", "items"), P("users")),
        check_vma=False,
    )
```

profile of v0, /device:TPU:1, one launch (start us, length us, event | category | flops | bytes accessed | tf_op | source)
XLA Modules:
  0.0 152.0 jit_solution(13896020500113062206)
XLA Ops:
  7.2 0.0 copy-start
  7.2 0.0 all-gather.2.cloned.1.call-start
  7.2 0.7 all-gather.2.cloned.1.call-update
  7.9 90.1 %all-gather.2.cloned.1.call-done = bf16[4096,8,128]{2,1,0:T(8,128)(2,1)} async-done(((bf16[64,8,128]{2,1,0:T(8,128)(2,1)}), bf16[4096,8,128]{2,1,0:T(8,128)(2,1)}) %all-gather.2.cloned.1.call-update) | async-done | bytes 8388624 | tf_op jit(solution)/shard_map/all_gather | solution.py:36
  98.0 0.0 copy-done
  98.0 21.6 %convolution_reduce_fusion = f32[32768]{0:T(1024)S(1)} fusion(bf16[1024,128]{1,0:T(8,128)(2,1)S(1)} %copy-done, bf16[4096,8,128]{2,1,0:T(8,128)(2,1)} %all-gather.2.cloned.1.call-done), kind=kOutput, calls=%fused_computation | convolution fusion | flops 8623456256 | bytes 8781824 | tf_op jit(solution)/shard_map/while/body/eval_jaxpr/dot_general | solution.py:27
  119.6 1.1 reduce_max.36
  120.7 0.6 reduce_max.37
  121.3 0.1 all_to_all.18
  121.4 15.0 %all_to_all.25 = f32[64,64,1]{1,2,0:T(1,128)S(1)} all-to-all(f32[64,64,1]{1,2,0:T(1,128)S(1)} %bitcast.10), channel_id=1, replica_groups=mesh['items'=4,'users'=64] {'users'}, dimensions={0} | all-to-all | bytes 32768 | tf_op jit(solution)/shard_map/all_to_all | solution.py:38
  136.4 0.1 reduce_max.38
  136.5 7.9 %all_to_all.26 = f32[4,1,64]{2,1,0:T(1,128)S(1)} all-to-all(f32[4,1,64]{2,1,0:T(1,128)S(1)} %broadcast_in_dim.5), channel_id=1, replica_groups=mesh['items'=4,'users'=64] {'items'}, dimensions={0} | all-to-all | bytes 2048 | tf_op jit(solution)/shard_map/all_to_all | solution.py:11
  144.4 0.0 copy-start.1
  144.4 0.7 copy.11
  145.1 0.0 copy-done.1
  (3 shorter events, 0.0 us)
Async XLA Ops:
  7.2 90.8 %copy-start = (bf16[1024,128]{1,0:T(8,128)(2,1)S(1)}, bf16[1024,128]{1,0:T(8,128)(2,1)}, u32[]{:S(2)}) copy-start(bf16[1024,128]{1,0:T(8,128)(2,1)} %param.3) | copy-start | bytes 786436
  7.2 90.8 %all-gather.2.cloned.1.call-start = ((), (), s32[]{:S(2)}) async-start(), calls=%async_computation.2 | async-start | bytes 8519680 | tf_op jit(solution)/shard_map/all_gather | solution.py:36
  144.4 0.7 copy-start.1
Sparse Core Ops, SparseCore 0:
  10.8 87.1 all-gather.1
where the time goes:
time: 152 us
  waiting for transfers between devices  90.8 us (60%)
  blocking collectives  22.9 us (15%)
  matrix products  21.6 us (14%)
  between operations  14.1 us (9%)
  local copies, waits for them, and re-layouts  1.92 us (1%)
    all_gather x1, waiting for transfers between devices, per_device(): everyone = lax.all_gather(capsules, 'users', axis=0, tiled=True)  90.1 us
    dot_general x1, matrix products, one_block(): lax.dot_general(flat, item_rows, (((1,), (1,)), ((), ())), preferred_elem...  21.6 us
    all_to_all x1, blocking collectives, per_device(): lax.all_to_all(own_block, 'users', split_axis=0, concat_axis=1, tiled=True)  15 us
    all_to_all x1, blocking collectives, sent_to_all(): lax.all_to_all(jnp.broadcast_to(value[None], (length, *value.shape)), axi...  7.9 us
  transfers between devices with their start and end apart: 1, of which 1 were waited for; matrix products, arithmetic and copies ran while one was open for 0% of the time, Pallas kernels for 0%

commit v1 on v0

v1 whole, which is shorter than its diff:
```python
import functools

import jax
import jax.numpy as jnp
from jax import lax
from jax.experimental import pallas as pl
from jax.experimental.pallas import tpu as pltpu
from jax.sharding import PartitionSpec as P

MESH = pl.DeviceIdType.MESH
NX, NY, NZ, NC = 4, 4, 8, 2
K, E, BLOCK = 8, 128, 1024
GROUP = 64
ROWS = GROUP * K
HALF = ROWS // 2
HB = BLOCK // 2

ORDER = (
    "uO00", "wp0", "uP00", "cp1", "uO10", "wp1", "cp2", "wc1", "uP10", "uP11", "uO20",
    "uO21", "wp2", "uP20", "uP21", "uO11", "cp3", "uO30", "wc2", "uO31", "uO32",
    "uP22", "cp4", "wp3", "uP30", "uP31", "uP32", "uO40", "wp4", "uP40", "uP41", "wc3",
    "uP42", "cp5", "uO50", "uO51", "uO52", "uO53", "cp6", "wp5", "uP50", "uP51",
    "uP52", "uP53", "wp6", "uP60", "uP61", "uP62", "uP63", "cp7", "uO70", "uO71",
    "uO72", "uO73", "uO60", "wp7", "uP70", "uP71", "uP72", "uP73", "uO61", "uO62",
    "uO63", "uP43", "uP33", "uO41", "uO42", "uO43", "uO33", "uP23", "uP12", "uP13",
    "uO22", "uO23", "uO12", "uO13", "uP01", "uP02", "uP03", "uO01", "uO02", "uO03",
)

COLUMNS = (((0, 0), (0, 1)), ((1, 0), (2, 1)), ((1, 1), (2, 0)), ((3, 0), (3, 1)))


def kernel(
    caps_ref, bank_ref, rel_ref, peak_ref,
    raw, tmp, own, par, bank, acc, res, recv, xsend, xrecv,
    load_sem, sr, rr, sl, rl, sp, rp, syr, ryr, syl, ryl, so, ro, sx, rx, xsem,
):
    x = lax.axis_index("items")
    u = lax.axis_index("users")
    c = u % 2
    y = (u // 2) % NY
    z = u // (2 * NY)

    def at(zz, yy, cc):
        return (x, (zz * NY + yy) * 2 + cc)

    z_up, z_dn = at((z + 1) % NZ, y, c), at((z + NZ - 1) % NZ, y, c)
    y_up, y_dn = at(z, (y + 1) % NY, c), at(z, (y + NY - 1) % NY, c)
    partner = at(z, y, 1 - c)
    x_peers = [((x + d) % NX, u) for d in (1, 3, 2)]

    def remote(src, dst, send, recv_, to):
        return pltpu.make_async_remote_copy(
            src_ref=src, dst_ref=dst, send_sem=send, recv_sem=recv_,
            device_id=to, device_id_type=MESH,
        )

    load_caps = pltpu.make_async_copy(caps_ref, raw, load_sem.at[0])
    load_bank = pltpu.make_async_copy(bank_ref, bank.at[0], load_sem.at[1])
    load_caps.start()
    load_bank.start()

    barrier = pltpu.get_barrier_semaphore()
    for to in (z_up, z_dn, y_up, y_dn, partner, x_peers[0], x_peers[1]):
        pl.semaphore_signal(barrier, inc=1, device_id=to, device_id_type=MESH)

    load_caps.wait()
    tmp[...] = raw[...].astype(jnp.float32).reshape(ROWS, E)
    for h in range(2):
        for k in range(K):
            rows = tmp[pl.ds(h * HALF + k, HALF // K, stride=K), :]
            own[0, pl.ds(h * HALF + k * (HALF // K), HALF // K), :] = rows.astype(
                jnp.bfloat16
            )
    load_bank.wait()
    pl.semaphore_wait(barrier, 7)

    a, b = pl.ds(0, HALF), pl.ds(HALF, HALF)
    up = {}
    down = {}

    def send_z(k, src_up, src_down):
        up[k] = remote(src_up, own.at[k, a], sr.at[k], rr.at[k], z_up)
        down[k] = remote(src_down, own.at[k, b], sl.at[k], rl.at[k], z_dn)
        up[k].start()
        down[k].start()

    over = {}

    def send_partner(k):
        over[k] = remote(own.at[k], par.at[k], sp.at[k], rp.at[k], partner)
        over[k].start()

    h0, h1 = pl.ds(0, HB), pl.ds(HB, HB)
    right = {}
    left = {}

    def send_y(i, src_up, dst_up, src_down, dst_down):
        right[i] = remote(src_up, dst_up, syr.at[i], ryr.at[i], y_up)
        left[i] = remote(src_down, dst_down, syl.at[i], ryl.at[i], y_dn)
        right[i].start()
        left[i].start()

    send_z(1, own.at[0, a], own.at[0, b])
    send_y(0, bank.at[0, h0], bank.at[1, h0], bank.at[0, h1], bank.at[2, h1])
    send_partner(0)
    send_z(2, own.at[0, b], own.at[0, a])
    send_y(1, bank.at[0, h1], bank.at[1, h1], bank.at[0, h0], bank.at[2, h0])
    for to in x_peers[:2]:
        pl.semaphore_signal(xsem, inc=1, device_id=to, device_id_type=MESH)

    seen = set()

    def unit(which, k, col):
        capsules = (own if which == 0 else par)[k]
        for j, h in COLUMNS[col]:
            items = bank[j, pl.ds(h * HB, HB), :]
            score = lax.dot_general(
                items, capsules, (((1,), (1,)), ((), ())),
                preferred_element_type=jnp.float32,
            )
            top = jnp.max(score.reshape(HB // 8, 8, ROWS), axis=0)
            for half in range(2):
                lo = half * HALF
                v = jnp.maximum(top[:, lo : lo + 128], top[:, lo + 128 : lo + 256])
                if (which, k, j) in seen:
                    v = jnp.maximum(v, acc[which, k, half, j])
                acc[which, k, half, j] = v
            seen.add((which, k, j))

    lane = lax.broadcasted_iota(jnp.int32, (8, 128), 1)
    row = lax.broadcasted_iota(jnp.int32, (8, 128), 0)
    block_row = [((y + d) % NY) * 2 + c for d in (0, 3, 1, 2)]

    def group_tile(which, first, second):
        halves = []
        for k, half in (first, second):
            v = jnp.full((8, 128), -jnp.inf, jnp.float32)
            for j in range(4):
                m = jnp.max(acc[which, k, half, j], axis=0, keepdims=True)
                v = jnp.where(row == block_row[j], m, v)
            v = jnp.maximum(v, pltpu.roll(v, 64, axis=1))
            halves.append(jnp.maximum(v, pltpu.roll(v, 32, axis=1)))
        return jnp.where(lane < 32, halves[0], halves[1])

    back = []

    def give_back(which, d, first, second):
        cc = c if which == 0 else 1 - c
        zz = (z + d) % NZ
        tile = group_tile(which, first, second)
        if which == 0 and d == 0:
            recv[z, c] = tile
            return
        i = len(back)
        res[i] = tile
        copy = remote(res.at[i], recv.at[z, c], so.at[i], ro.at[z, c], at(zz, y, cc))
        copy.start()
        back.append(copy)

    left_to_do = {}
    for op in ORDER:
        if op[0] == "u":
            key = (op[1], (int(op[2]) + 1) // 2)
            left_to_do[key] = left_to_do.get(key, 0) + 1

    for op in ORDER:
        if op[:2] == "cp":
            k = int(op[2])
            up[k].wait_recv()
            down[k].wait_recv()
            if k <= 5:
                send_z(k + 2, own.at[k, a], own.at[k, b])
            send_partner(k)
        elif op[:2] == "wp":
            over[int(op[2])].wait_recv()
        elif op[:2] == "wc":
            i = int(op[2]) - 1
            right[i].wait_recv()
            left[i].wait_recv()
            if i == 0:
                send_y(2, bank.at[1, h0], bank.at[3, h0], bank.at[2, h1], bank.at[3, h1])
        else:
            which, k, col = "OP".index(op[1]), int(op[2]), int(op[3])
            unit(which, k, col)
            d = (k + 1) // 2
            left_to_do[(op[1], d)] -= 1
            if left_to_do[(op[1], d)] == 0:
                if d == 0:
                    give_back(which, 0, (0, 0), (0, 1))
                elif d == 4:
                    give_back(which, 4, (7, 0), (7, 1))
                else:
                    give_back(which, NZ - d, (2 * d - 1, 0), (2 * d, 0))
                    give_back(which, d, (2 * d, 1), (2 * d - 1, 1))

    for dz in range(NZ):
        for dc in range(NC):
            if dz or dc:
                zz, cc = (z + dz) % NZ, (c + dc) % 2
                remote(
                    res.at[0], recv.at[zz, cc], so.at[0], ro.at[zz, cc], partner
                ).wait_recv()
    table = jnp.maximum(recv[:, 0], recv[:, 1])
    top = jnp.max(jnp.max(table, axis=0), axis=0, keepdims=True)
    xsend[...] = jnp.broadcast_to(top, (8, 128))
    pl.semaphore_wait(xsem, 2)
    over_x = [
        remote(xsend, xrecv.at[i], sx.at[i], rx.at[i], to)
        for i, to in enumerate(x_peers)
    ]
    for copy in over_x:
        copy.start()
    for copy in over_x:
        copy.wait_recv()
    peak = jnp.maximum(
        jnp.maximum(xsend[...], xrecv[0]), jnp.maximum(xrecv[1], xrecv[2])
    )
    relative = (table - peak[None]).reshape(NZ * 8, 128)
    rel_ref[...] = relative.T[:GROUP, :]
    peak_ref[...] = peak[:1, :]

    for copies in (up, down, over, right, left):
        for copy in copies.values():
            copy.wait_send()
    for copy in back + over_x:
        copy.wait_send()


def per_device(capsules, bank):
    vmem = pltpu.VMEM
    dma = pltpu.SemaphoreType.DMA
    relative, peak = pl.pallas_call(
        kernel,
        out_shape=(
            jax.ShapeDtypeStruct((GROUP, NZ * 8), jnp.float32),
            jax.ShapeDtypeStruct((1, 128), jnp.float32),
        ),
        in_specs=[pl.BlockSpec(memory_space=pl.ANY)] * 2,
        out_specs=(
            pl.BlockSpec(memory_space=pltpu.VMEM),
            pl.BlockSpec(memory_space=pltpu.VMEM),
        ),
        scratch_shapes=[
            vmem((GROUP, K, E), jnp.bfloat16),
            vmem((ROWS, E), jnp.float32),
            vmem((8, ROWS, E), jnp.bfloat16),
            vmem((8, ROWS, E), jnp.bfloat16),
            vmem((4, BLOCK, E), jnp.bfloat16),
            vmem((2, 8, 2, 4, 8, 128), jnp.float32),
            vmem((15, 8, 128), jnp.float32),
            vmem((NZ, NC, 8, 128), jnp.float32),
            vmem((8, 128), jnp.float32),
            vmem((3, 8, 128), jnp.float32),
            dma((2,)),
            dma((8,)), dma((8,)), dma((8,)), dma((8,)), dma((8,)), dma((8,)),
            dma((3,)), dma((3,)), dma((3,)), dma((3,)),
            dma((15,)), dma((NZ, NC)),
            dma((3,)), dma((3,)),
            pltpu.SemaphoreType.REGULAR,
        ],
        compiler_params=pltpu.CompilerParams(collective_id=0, has_side_effects=True),
    )(capsules, bank)
    return relative, peak[0, :GROUP]


def solution(mesh):
    return jax.shard_map(
        per_device,
        mesh=mesh,
        in_specs=(P("users", None, None), P(("items", "users"), None)),
        out_specs=(P("users", "items"), P("users")),
        check_vma=False,
    )
```

time: 152 us -> 45.4 us (0.30)
  waiting for transfers between devices: 90.8 us -> 0 us
  Pallas kernels: 0 us -> 42.1 us
  blocking collectives: 22.9 us -> 0 us
  matrix products: 21.6 us -> 0 us
  between operations: 14.1 us -> 0.65 us
    all_gather x1 -> x0, waiting for transfers between devices: 90.1 us -> none  [per_device(): everyone = lax.all_gather(capsules, 'users', axis=0, tiled=True)]
    pallas_call x0 -> x1, Pallas kernels: none -> 42.1 us  [per_device(): pl.pallas_call(kernel, out_shape=(jax.ShapeDtypeStruct((GROUP, NZ * 8), j...]
    all_to_all x2 -> x0, blocking collectives: 22.9 us -> none  [the longest x1 15 us: per_device(): lax.all_to_all(own_block, 'users', split_axis=0, concat_axis=1, tiled=True)]
    dot_general x1 -> x0, matrix products: 21.6 us -> none  [one_block(): lax.dot_general(flat, item_rows, (((1,), (1,)), ((), ())), preferred_elem...]
  transfers between devices with their start and end apart: 1 -> 0, of which waited for: 1 -> 0; matrix products, arithmetic and copies ran while one was open for 0% -> 0% of each run, Pallas kernels for 0% -> 0%
where the time goes in v1:
time: 45.4 us; the launch traced here: 45.2 us
  Pallas kernels  42.1 us (93%)
  local copies, waits for them, and re-layouts  2.51 us (6%)
  between operations  0.65 us (1%)
    pallas_call x1, Pallas kernels, per_device(): pl.pallas_call(kernel, out_shape=(jax.ShapeDtypeStruct((GROUP, NZ * 8), j...  42.1 us
    unnamed x3, local copies, waits for them, and re-layouts  2 us

profile of v1, /device:TPU:1, one launch (start us, length us, event | category | flops | bytes accessed | tf_op | source)
XLA Modules:
  0.0 45.2 jit_solution(735559206337492312)
XLA Ops:
  0.6 42.1 %shard_map.41 = (f32[64,64]{1,0:T(8,128)}, f32[1,128]{1,0:T(1,128)}) custom-call(bf16[64,8,128]{2,1,0:T(8,128)(2,1)} %caps_ref.1, bf16[1024,128]{1,0:T(8,128)(2,1)} %bank_ref.1), custom_call_target="tpu_custom_call" | custom-call | tf_op jit(solution)/shard_map/pallas_call | solution.py:232
  42.7 0.0 copy-start
  42.7 0.6 %copy-done = f32[1,128]{1,0:T(1,128)S(1)} copy-done((f32[1,128]{1,0:T(1,128)S(1)}, f32[1,128]{1,0:T(1,128)}, u32[]{:S(2)}) %copy-start) | copy-done | bytes 536
  43.3 0.5 %slice_bitcast_fusion = f32[64]{0:T(128)} fusion(f32[1,128]{1,0:T(1,128)S(1)} %copy-done), kind=kLoop, calls=%fused_computation | loop fusion | bytes 512 | tf_op jit(solution)/shard_map/squeeze | solution.py:263
  43.8 1.4 %copy.5 = f32[64,64]{1,0:T(8,128)} copy(f32[64,64]{1,0:T(8,128)} %get-tuple-element.8) | data formatting | bytes 32768
Async XLA Ops:
  42.7 0.6 %copy-start = (f32[1,128]{1,0:T(1,128)S(1)}, f32[1,128]{1,0:T(1,128)}, u32[]{:S(2)}) copy-start(f32[1,128]{1,0:T(1,128)} %get-tuple-element.5) | copy-start | bytes 1540

commit v2 on v1

v2 whole, which is shorter than its diff:
```python
import jax
import jax.numpy as jnp
from jax import lax
from jax.experimental import pallas as pl
from jax.experimental.pallas import tpu as pltpu
from jax.sharding import PartitionSpec as P

MESH = pl.DeviceIdType.MESH
NX, NY, NZ, NC = 4, 4, 8, 2
K, E, BLOCK = 8, 128, 1024
GROUP = 64
ROWS = GROUP * K
HALF = ROWS // 2
QB = BLOCK // 4

SEGMENTS = (
    ((), ("O0:0",)),
    (("p0",), ("P0:0",)),
    (("o1", "c1",), ("O1:01",)),
    ((), ("P0:1", "O0:1",)),
    (("p1",), ("P1:01",)),
    (("o2", "c2",), ("O2:012", "P1:2", "O1:2",)),
    ((), ("P0:2", "O0:2",)),
    (("c3", "p2",), ("P2:0123", "O2:3", "P1:3", "O1:3",)),
    (("o3", "c4",), ("O3:01234", "P2:4", "O2:4", "P1:4", "O1:4",)),
    (("o4", "c5", "p3",), ("O4:012345", "P3:012",)),
    (("c6", "p4",), ("P4:0123456", "O4:6", "P3:34",)),
    (("o5",), ("O5:0123456", "P3:56", "O3:5",)),
    (("o6", "p5",), ("O6:0123456", "P5:01",)),
    (("p6",), ("P6:0123456", "P5:234",)),
    (("o7",), ("O7:0123456", "P5:56", "O3:6",)),
    (("p7",), ("P7:0123456", "P2:56", "O2:5",)),
    ((), ("O2:6", "P1:56", "O1:56",)),
    ((), ("P0:3456",)),
    ((), ("O0:3456",)),
)

COLUMNS = (
    ((0, 0, BLOCK),),
    ((1, 0, QB), (2, 3 * QB, QB)),
    ((1, QB, QB), (2, 2 * QB, QB)),
    ((1, 2 * QB, QB), (2, QB, QB)),
    ((1, 3 * QB, QB), (2, 0, QB)),
    ((3, 0, QB), (3, 3 * QB, QB)),
    ((3, QB, QB), (3, 2 * QB, QB)),
)


def groups_of(d):
    if d == 0:
        return ((0, (0, 0), (0, 1)),)
    if d == 4:
        return ((4, (7, 0), (7, 1)),)
    lo, hi = 2 * d - 1, 2 * d
    return ((NZ - d, (lo, 0), (hi, 0)), (d, (hi, 1), (lo, 1)))


def kernel(
    caps_ref, bank_ref, rel_ref, peak_ref,
    raw, tmp, own, par, bank, acc, res, recv, xsend, xrecv,
    load_sem, sr, rr, sl, rl, sp, rp, syr, ryr, syl, ryl, so, ro, sx, rx, xsem,
):
    x = lax.axis_index("items")
    u = lax.axis_index("users")
    c = lax.rem(u, NC)
    y = lax.rem(lax.div(u, NC), NY)
    z = lax.div(u, NC * NY)

    def at(zz, yy, cc):
        return (x, (zz * NY + yy) * NC + cc)

    def turn(i, d, n):
        return lax.rem(i + d, n)

    z_up, z_dn = at(turn(z, 1, NZ), y, c), at(turn(z, NZ - 1, NZ), y, c)
    y_up, y_dn = at(z, turn(y, 1, NY), c), at(z, turn(y, NY - 1, NY), c)
    partner = at(z, y, 1 - c)
    x_peers = [(turn(x, d, NX), u) for d in (1, 3, 2)]

    def remote(src, dst, send, recv_, to):
        return pltpu.make_async_remote_copy(
            src_ref=src, dst_ref=dst, send_sem=send, recv_sem=recv_,
            device_id=to, device_id_type=MESH,
        )

    load_caps = pltpu.make_async_copy(caps_ref, raw, load_sem.at[0])
    load_bank = pltpu.make_async_copy(bank_ref, bank.at[0], load_sem.at[1])
    load_caps.start()
    load_bank.start()

    barrier = pltpu.get_barrier_semaphore()
    for to in (z_up, z_dn, y_up, y_dn, partner, x_peers[0], x_peers[1]):
        pl.semaphore_signal(barrier, inc=1, device_id=to, device_id_type=MESH)

    load_caps.wait()
    tmp[...] = raw[...].astype(jnp.float32).reshape(ROWS, E)
    for h in range(2):
        for k in range(K):
            rows = tmp[pl.ds(h * HALF + k, HALF // K, stride=K), :]
            own[0, pl.ds(h * HALF + k * (HALF // K), HALF // K), :] = rows.astype(
                jnp.bfloat16
            )
    load_bank.wait()
    pl.semaphore_wait(barrier, 7)

    a, b = pl.ds(0, HALF), pl.ds(HALF, HALF)
    up, down, over, right, left = {}, {}, {}, {}, {}

    def send_z(k, src_up, src_down):
        up[k] = remote(src_up, own.at[k, a], sr.at[k], rr.at[k], z_up)
        down[k] = remote(src_down, own.at[k, b], sl.at[k], rl.at[k], z_dn)
        up[k].start()
        down[k].start()

    def send_partner(k):
        over[k] = remote(own.at[k], par.at[k], sp.at[k], rp.at[k], partner)
        over[k].start()

    def send_y(col, from_up, from_down):
        to_up, to_down = COLUMNS[col]
        slot_up = bank.at[to_up[0], pl.ds(to_up[1], QB)]
        slot_down = bank.at[to_down[0], pl.ds(to_down[1], QB)]
        src_up = bank.at[from_up, pl.ds(to_up[1], QB)]
        src_down = bank.at[from_down, pl.ds(to_down[1], QB)]
        right[col] = remote(src_up, slot_up, syr.at[col], ryr.at[col], y_up)
        left[col] = remote(src_down, slot_down, syl.at[col], ryl.at[col], y_dn)
        right[col].start()
        left[col].start()

    send_z(1, own.at[0, a], own.at[0, b])
    send_y(1, 0, 0)
    send_partner(0)
    send_z(2, own.at[0, b], own.at[0, a])
    for col in (2, 3, 4):
        send_y(col, 0, 0)
    for to in x_peers[:2]:
        pl.semaphore_signal(xsem, inc=1, device_id=to, device_id_type=MESH)

    seen = set()

    def score_slot(which, k, cols):
        pieces = [p for col in cols for p in COLUMNS[col]]
        items = [bank[j, pl.ds(lo, n), :] for j, lo, n in pieces]
        score = lax.dot_general(
            items[0] if len(items) == 1 else jnp.concatenate(items, axis=0),
            (own if which == 0 else par)[k],
            (((1,), (1,)), ((), ())),
            preferred_element_type=jnp.float32,
        )
        tops, start = {}, 0
        for j, _, n in pieces:
            part = score[start : start + n].reshape(n // 8, 8, ROWS)
            top = jnp.max(part, axis=0)
            tops[j] = jnp.maximum(tops[j], top) if j in tops else top
            start += n
        for j, top in tops.items():
            for half in range(2):
                lo = half * HALF
                v = jnp.maximum(top[:, lo : lo + 128], top[:, lo + 128 : lo + 256])
                if (which, k, j) in seen:
                    v = jnp.maximum(v, acc[which, k, half, j])
                acc[which, k, half, j] = v
            seen.add((which, k, j))

    lane = lax.broadcasted_iota(jnp.int32, (8, 128), 1)
    row = lax.broadcasted_iota(jnp.int32, (8, 128), 0)
    block_row = [turn(y, d, NY) * NC + c for d in (0, 3, 1, 2)]

    def group_tile(which, first, second):
        halves = []
        for k, half in (first, second):
            v = jnp.full((8, 128), -jnp.inf, jnp.float32)
            for j in range(4):
                m = jnp.max(acc[which, k, half, j], axis=0, keepdims=True)
                v = jnp.where(row == block_row[j], m, v)
            v = jnp.maximum(v, pltpu.roll(v, 64, axis=1))
            halves.append(jnp.maximum(v, pltpu.roll(v, 32, axis=1)))
        return jnp.where(lane < 32, halves[0], halves[1])

    back = []
    to_send = []

    def finish(which, d):
        cc = c if which == 0 else 1 - c
        for dz, first, second in groups_of(d):
            tile = group_tile(which, first, second)
            if which == 0 and d == 0:
                recv[z, c] = tile
                continue
            i = len(back)
            res[i] = tile
            to = at(turn(z, dz, NZ), y, cc)
            back.append(remote(res.at[i], recv.at[z, c], so.at[i], ro.at[z, c], to))
            to_send.append(back[-1])

    def event(name):
        i = int(name[1])
        if name[0] == "o":
            up[i].wait_recv()
            down[i].wait_recv()
        elif name[0] == "p":
            over[i].wait_recv()
        else:
            right[i].wait_recv()
            left[i].wait_recv()

    def pass_on(name):
        i = int(name[1])
        if name[0] == "o":
            if i <= 5:
                send_z(i + 2, own.at[i, a], own.at[i, b])
            send_partner(i)
        elif name[0] == "c" and i <= 2:
            send_y(i + 4, 1, 2)

    left_over = {}
    for _, units in SEGMENTS:
        for unit in units:
            key = (unit[0], (int(unit[1]) + 1) // 2)
            left_over[key] = left_over.get(key, 0) + len(unit) - 3
    done = []
    for names, units in SEGMENTS:
        for name in names:
            event(name)
        for name in names:
            pass_on(name)
        for copy in to_send:
            copy.start()
        to_send.clear()
        for key in done:
            finish(*key)
        done.clear()
        for unit in units:
            which, k = "OP".index(unit[0]), int(unit[1])
            score_slot(which, k, [int(i) for i in unit[3:]])
            key = (unit[0], (k + 1) // 2)
            left_over[key] -= len(unit) - 3
            if not left_over[key]:
                done.append((which, key[1]))
    for copy in to_send:
        copy.start()
    to_send.clear()
    for key in done:
        finish(*key)

    for dz in range(NZ):
        for dc in range(NC):
            if dz or dc:
                zz, cc = turn(z, dz, NZ), turn(c, dc, NC)
                remote(
                    res.at[0], recv.at[zz, cc], so.at[0], ro.at[zz, cc], partner
                ).wait_recv()
    table = jnp.maximum(recv[:, 0], recv[:, 1])
    top = jnp.max(jnp.max(table, axis=0), axis=0, keepdims=True)
    xsend[...] = jnp.broadcast_to(top, (8, 128))
    pl.semaphore_wait(xsem, 2)
    over_x = [
        remote(xsend, xrecv.at[i], sx.at[i], rx.at[i], to)
        for i, to in enumerate(x_peers)
    ]
    for copy in over_x:
        copy.start()
    for copies in (up, down, over, right, left):
        for copy in copies.values():
            copy.wait_send()
    for copy in back:
        copy.wait_send()
    for copy in over_x:
        copy.wait_recv()
    peak = jnp.maximum(
        jnp.maximum(xsend[...], xrecv[0]), jnp.maximum(xrecv[1], xrecv[2])
    )
    relative = (table - peak[None]).reshape(NZ * 8, 128)
    rel_ref[...] = relative.T[:GROUP, :]
    peak_ref[...] = peak[:1, :]
    for copy in over_x:
        copy.wait_send()


def flush(rel_ref, peak_ref, rel_out, peak_out, row, sem):
    first = pltpu.make_async_copy(rel_ref, rel_out, sem.at[0])
    first.start()
    row[...] = peak_ref[0, :GROUP]
    second = pltpu.make_async_copy(row, peak_out, sem.at[1])
    second.start()
    first.wait()
    second.wait()


def per_device(capsules, bank):
    vmem = pltpu.VMEM
    dma = pltpu.SemaphoreType.DMA
    whole = pl.BlockSpec(memory_space=pltpu.VMEM)
    anywhere = pl.BlockSpec(memory_space=pl.ANY)
    relative, peak = pl.pallas_call(
        kernel,
        out_shape=(
            vmem((GROUP, NZ * 8), jnp.float32),
            vmem((1, 128), jnp.float32),
        ),
        in_specs=[anywhere] * 2,
        out_specs=(whole, whole),
        scratch_shapes=[
            vmem((GROUP, K, E), jnp.bfloat16),
            vmem((ROWS, E), jnp.float32),
            vmem((8, ROWS, E), jnp.bfloat16),
            vmem((8, ROWS, E), jnp.bfloat16),
            vmem((4, BLOCK, E), jnp.bfloat16),
            vmem((2, 8, 2, 4, 8, 128), jnp.float32),
            vmem((15, 8, 128), jnp.float32),
            vmem((NZ, NC, 8, 128), jnp.float32),
            vmem((8, 128), jnp.float32),
            vmem((3, 8, 128), jnp.float32),
            dma((2,)),
            dma((8,)), dma((8,)), dma((8,)), dma((8,)), dma((8,)), dma((8,)),
            dma((7,)), dma((7,)), dma((7,)), dma((7,)),
            dma((15,)), dma((NZ, NC)),
            dma((3,)), dma((3,)),
            pltpu.SemaphoreType.REGULAR,
        ],
        compiler_params=pltpu.CompilerParams(collective_id=0, has_side_effects=True),
    )(capsules, bank)
    return pl.pallas_call(
        flush,
        out_shape=(
            jax.ShapeDtypeStruct((GROUP, NZ * 8), jnp.float32),
            jax.ShapeDtypeStruct((GROUP,), jnp.float32),
        ),
        in_specs=[whole, whole],
        out_specs=(anywhere, anywhere),
        scratch_shapes=[vmem((GROUP,), jnp.float32), dma((2,))],
    )(
        pltpu.with_memory_space_constraint(relative, pltpu.VMEM),
        pltpu.with_memory_space_constraint(peak, pltpu.VMEM),
    )


def solution(mesh):
    return jax.shard_map(
        per_device,
        mesh=mesh,
        in_specs=(P("users", None, None), P(("items", "users"), None)),
        out_specs=(P("users", "items"), P("users")),
        check_vma=False,
    )
```

time: 45.4 us -> 42 us (0.925)
  local copies, waits for them, and re-layouts: 2.51 us -> 0 us
  Pallas kernels: 42.1 us -> 41.1 us
    unnamed x3 -> x0, local copies, waits for them, and re-layouts: 2 us -> none
    pallas_call x1 -> x2, Pallas kernels: 42.1 us -> 41.1 us  [the longest x1 40.5 us: per_device(): pl.pallas_call(kernel, out_shape=(vmem((GROUP, NZ * 8), jnp.float32), vme...]
    squeeze x1 -> x0, local copies, waits for them, and re-layouts: 0.51 us -> none  [per_device(): return (relative, peak[0, :GROUP])]
where the time goes in v2:
time: 42 us; the launch traced here: 41.9 us
  Pallas kernels  41.1 us (98%)
  between operations  0.8 us (2%)
    pallas_call x1, Pallas kernels, per_device(): pl.pallas_call(kernel, out_shape=(vmem((GROUP, NZ * 8), jnp.float32), vme...  40.5 us

profile of v2, /device:TPU:1, one launch (start us, length us, event | category | flops | bytes accessed | tf_op | source)
XLA Modules:
  0.0 41.9 jit_solution(16711042086785856750)
XLA Ops:
  0.6 40.5 %shard_map.41 = (f32[64,64]{1,0:T(8,128)S(1)}, f32[1,128]{1,0:T(1,128)S(1)}) custom-call(bf16[64,8,128]{2,1,0:T(8,128)(2,1)} %caps_ref.1, bf16[1024,128]{1,0:T(8,128)(2,1)} %bank_ref.1), custom_call_target="tpu_custom_call" | custom-call | tf_op jit(solution)/shard_map/pallas_call | solution.py:295
  41.1 0.6 %shard_map.42 = (f32[64,64]{1,0:T(8,128)}, f32[64]{0:T(128)}) custom-call(f32[64,64]{1,0:T(8,128)S(1)} %get-tuple-element.4.rel_ref, f32[1,128]{1,0:T(1,128)S(1)} %get-tuple-element.5.peak_ref), custom_call_target="tpu_custom_call" | custom-call | tf_op jit(solution)/shard_map/pallas_call | solution.py:323

commit v3 on v2

--- a/solution.py
+++ b/solution.py
@@ -12,6 +12,9 @@
 ROWS = GROUP * K
 HALF = ROWS // 2
 QB = BLOCK // 4
+TILE = 256
+DEPTH = 4
+LAG = 2
 
 SEGMENTS = (
     ((), ("O0:0",)),
@@ -21,16 +24,22 @@
     (("p1",), ("P1:01",)),
     (("o2", "c2",), ("O2:012", "P1:2", "O1:2",)),
     ((), ("P0:2", "O0:2",)),
-    (("c3", "p2",), ("P2:0123", "O2:3", "P1:3", "O1:3",)),
-    (("o3", "c4",), ("O3:01234", "P2:4", "O2:4", "P1:4", "O1:4",)),
-    (("o4", "c5", "p3",), ("O4:012345", "P3:012",)),
-    (("c6", "p4",), ("P4:0123456", "O4:6", "P3:34",)),
-    (("o5",), ("O5:0123456", "P3:56", "O3:5",)),
-    (("o6", "p5",), ("O6:0123456", "P5:01",)),
-    (("p6",), ("P6:0123456", "P5:234",)),
-    (("o7",), ("O7:0123456", "P5:56", "O3:6",)),
-    (("p7",), ("P7:0123456", "P2:56", "O2:5",)),
-    ((), ("O2:6", "P1:56", "O1:56",)),
+    (("c3",), ("O2:3", "P1:3", "O1:3",)),
+    (("p2",), ("P2:0123",)),
+    (("o3", "c4",), ("O3:01234", "P2:4",)),
+    ((), ("O2:4", "P1:4", "O1:4",)),
+    (("o4", "c5", "p3",), ("O4:012345",)),
+    ((), ("P3:012345",)),
+    (("c6", "p4",), ("O3:5", "P4:01234",)),
+    (("o5",), ("P4:5", "O5:01234",)),
+    (("o6",), ("O5:5", "O6:01234",)),
+    (("p5",), ("O6:56", "P5:0123",)),
+    (("p6",), ("P5:4", "P6:01234",)),
+    ((), ("P6:56", "P5:56", "O5:6", "P4:6", "O4:6",)),
+    (("o7",), ("P3:6", "O7:01234",)),
+    ((), ("O7:56", "O3:6", "P2:56", "O2:56",)),
+    (("p7",), ("P1:5", "P7:01234",)),
+    ((), ("P7:56", "P1:6", "O1:56",)),
     ((), ("P0:3456",)),
     ((), ("O0:3456",)),
 )
@@ -58,7 +67,25 @@
 def kernel(
     caps_ref, bank_ref, rel_ref, peak_ref,
     raw, tmp, own, par, bank, acc, res, recv, xsend, xrecv,
-    load_sem, sr, rr, sl, rl, sp, rp, syr, ryr, syl, ryl, so, ro, sx, rx, xsem,
+    load_sem, sent, came_z, came_p, came_y, came_back, came_x, xsem,
+):
+    def body(*sums):
+        score_blocks(
+            caps_ref, bank_ref, rel_ref, peak_ref,
+            raw, tmp, own, par, bank, acc, res, recv, xsend, xrecv,
+            load_sem, sent, came_z, came_p, came_y, came_back, came_x, xsem,
+            (sums[:DEPTH], sums[DEPTH:]),
+        )
+
+    tile = [pltpu.ACC(q)((TILE, 2 * E), jnp.float32) for q in (0, 1)]
+    pl.run_scoped(body, *[tile[0]] * DEPTH, *[tile[1]] * DEPTH)
+
+
+def score_blocks(
+    caps_ref, bank_ref, rel_ref, peak_ref,
+    raw, tmp, own, par, bank, acc, res, recv, xsend, xrecv,
+    load_sem, sent, came_z, came_p, came_y, came_back, came_x, xsem,
+    sums,
 ):
     x = lax.axis_index("items")
     u = lax.axis_index("users")
@@ -104,17 +131,16 @@
     pl.semaphore_wait(barrier, 7)
 
     a, b = pl.ds(0, HALF), pl.ds(HALF, HALF)
-    up, down, over, right, left = {}, {}, {}, {}, {}
 
     def send_z(k, src_up, src_down):
-        up[k] = remote(src_up, own.at[k, a], sr.at[k], rr.at[k], z_up)
-        down[k] = remote(src_down, own.at[k, b], sl.at[k], rl.at[k], z_dn)
-        up[k].start()
-        down[k].start()
+        up = remote(src_up, own.at[k, a], sent.at[0], came_z.at[k], z_up)
+        down = remote(src_down, own.at[k, b], sent.at[0], came_z.at[k], z_dn)
+        up.start()
+        down.start()
 
     def send_partner(k):
-        over[k] = remote(own.at[k], par.at[k], sp.at[k], rp.at[k], partner)
-        over[k].start()
+        over = remote(own.at[k], par.at[k], sent.at[1], came_p.at[k], partner)
+        over.start()
 
     def send_y(col, from_up, from_down):
         to_up, to_down = COLUMNS[col]
@@ -122,10 +148,10 @@
         slot_down = bank.at[to_down[0], pl.ds(to_down[1], QB)]
         src_up = bank.at[from_up, pl.ds(to_up[1], QB)]
         src_down = bank.at[from_down, pl.ds(to_down[1], QB)]
-        right[col] = remote(src_up, slot_up, syr.at[col], ryr.at[col], y_up)
-        left[col] = remote(src_down, slot_down, syl.at[col], ryl.at[col], y_dn)
-        right[col].start()
-        left[col].start()
+        right = remote(src_up, slot_up, sent.at[2], came_y.at[col], y_up)
+        left = remote(src_down, slot_down, sent.at[2], came_y.at[col], y_dn)
+        right.start()
+        left.start()
 
     send_z(1, own.at[0, a], own.at[0, b])
     send_y(1, 0, 0)
@@ -138,29 +164,39 @@
 
     seen = set()
 
-    def score_slot(which, k, cols):
-        pieces = [p for col in cols for p in COLUMNS[col]]
-        items = [bank[j, pl.ds(lo, n), :] for j, lo, n in pieces]
-        score = lax.dot_general(
-            items[0] if len(items) == 1 else jnp.concatenate(items, axis=0),
-            (own if which == 0 else par)[k],
-            (((1,), (1,)), ((), ())),
-            preferred_element_type=jnp.float32,
-        )
-        tops, start = {}, 0
-        for j, _, n in pieces:
-            part = score[start : start + n].reshape(n // 8, 8, ROWS)
-            top = jnp.max(part, axis=0)
-            tops[j] = jnp.maximum(tops[j], top) if j in tops else top
-            start += n
-        for j, top in tops.items():
-            for half in range(2):
-                lo = half * HALF
-                v = jnp.maximum(top[:, lo : lo + 128], top[:, lo + 128 : lo + 256])
-                if (which, k, j) in seen:
-                    v = jnp.maximum(v, acc[which, k, half, j])
-                acc[which, k, half, j] = v
-            seen.add((which, k, j))
+    zeros = jnp.zeros((TILE, E), jnp.bfloat16)
+    flying = []
+    count = [0, 0]
+
+    def push(which, k):
+        for q in range(2):
+            rows = (own if which == 0 else par)[k, pl.ds(q * HALF, HALF), :]
+            pltpu.matmul_push_rhs(
+                jnp.concatenate([rows, rows], axis=1),
+                staging_register=count[1] % 2, mxu_index=q, transpose=True,
+            )
+        count[1] += 1
+
+    def read_oldest():
+        i, which, k, j = flying.pop(0)
+        for half in range(2):
+            score = pltpu.matmul_pop(sums[half][i])
+            top = jnp.max(score.reshape(TILE // 8, 8, 2 * E), axis=0)
+            v = jnp.maximum(top[:, :E], top[:, E:])
+            if (which, k, j) in seen:
+                v = jnp.maximum(v, acc[which, k, half, j])
+            acc[which, k, half, j] = v
+        seen.add((which, k, j))
+
+    def multiply(which, k, j, lo, register):
+        i = count[0] % DEPTH
+        items = jnp.concatenate([bank[j, pl.ds(lo, TILE), :], zeros], axis=1)
+        for q in range(2):
+            pltpu.matmul_acc_lhs(sums[q][i], items, load_staged_rhs=register)
+        count[0] += 1
+        flying.append((i, which, k, j))
+        if len(flying) > LAG:
+            read_oldest()
 
     lane = lax.broadcasted_iota(jnp.int32, (8, 128), 1)
     row = lax.broadcasted_iota(jnp.int32, (8, 128), 0)
@@ -190,19 +226,23 @@
             i = len(back)
             res[i] = tile
             to = at(turn(z, dz, NZ), y, cc)
-            back.append(remote(res.at[i], recv.at[z, c], so.at[i], ro.at[z, c], to))
+            back.append(remote(res.at[i], recv.at[z, c], sent.at[3], came_back, to))
             to_send.append(back[-1])
+
+    def landed(ref, sem):
+        remote(ref, ref, sent.at[0], sem, partner).wait_recv()
+
+    def left_here(ref, sem):
+        remote(ref, ref, sem, came_back, partner).wait_send()
 
     def event(name):
         i = int(name[1])
         if name[0] == "o":
-            up[i].wait_recv()
-            down[i].wait_recv()
+            landed(own.at[i], came_z.at[i])
         elif name[0] == "p":
-            over[i].wait_recv()
+            landed(par.at[i], came_p.at[i])
         else:
-            right[i].wait_recv()
-            left[i].wait_recv()
+            landed(bank.at[0, pl.ds(0, 2 * QB)], came_y.at[i])
 
     def pass_on(name):
         i = int(name[1])
@@ -213,13 +253,29 @@
         elif name[0] == "c" and i <= 2:
             send_y(i + 4, 1, 2)
 
+    visits = []
+    for n, (_, units) in enumerate(SEGMENTS):
+        for unit in units:
+            tiles = [
+                (j, lo + t)
+                for col in unit[3:]
+                for j, lo, rows in COLUMNS[int(col)]
+                for t in range(0, rows, TILE)
+            ]
+            visits.append((n, "OP".index(unit[0]), int(unit[1]), tiles))
     left_over = {}
-    for _, units in SEGMENTS:
-        for unit in units:
-            key = (unit[0], (int(unit[1]) + 1) // 2)
-            left_over[key] = left_over.get(key, 0) + len(unit) - 3
+    for _, which, k, tiles in visits:
+        key = (which, (k + 1) // 2)
+        left_over[key] = left_over.get(key, 0) + len(tiles)
+    arrives = {(0, 0): -1}
+    for n, (names, _) in enumerate(SEGMENTS):
+        for name in names:
+            if name[0] != "c":
+                arrives["op".index(name[0]), int(name[1])] = n
     done = []
-    for names, units in SEGMENTS:
+    pushed = 0
+    at_visit = 0
+    for n, (names, units) in enumerate(SEGMENTS):
         for name in names:
             event(name)
         for name in names:
@@ -227,54 +283,60 @@
         for copy in to_send:
             copy.start()
         to_send.clear()
-        for key in done:
-            finish(*key)
-        done.clear()
-        for unit in units:
-            which, k = "OP".index(unit[0]), int(unit[1])
-            score_slot(which, k, [int(i) for i in unit[3:]])
-            key = (unit[0], (k + 1) // 2)
-            left_over[key] -= len(unit) - 3
+        ready, done = done, []
+        while at_visit < len(visits) and visits[at_visit][0] == n:
+            _, which, k, tiles = visits[at_visit]
+            if pushed == at_visit:
+                push(which, k)
+                pushed += 1
+            register = at_visit % 2
+            for t, (j, lo) in enumerate(tiles):
+                multiply(which, k, j, lo, None if t else register)
+                if not t and at_visit + 1 < len(visits):
+                    after = visits[at_visit + 1][1:3]
+                    if arrives[after] <= n:
+                        push(*after)
+                        pushed += 1
+                if len(ready) and t == 1:
+                    for key in ready:
+                        finish(*key)
+                    ready = []
+            key = (which, (k + 1) // 2)
+            left_over[key] -= len(tiles)
             if not left_over[key]:
-                done.append((which, key[1]))
+                done.append(key)
+            at_visit += 1
+    while flying:
+        read_oldest()
     for copy in to_send:
         copy.start()
     to_send.clear()
     for key in done:
         finish(*key)
 
-    for dz in range(NZ):
-        for dc in range(NC):
-            if dz or dc:
-                zz, cc = turn(z, dz, NZ), turn(c, dc, NC)
-                remote(
-                    res.at[0], recv.at[zz, cc], so.at[0], ro.at[zz, cc], partner
-                ).wait_recv()
+    landed(res, came_back)
     table = jnp.maximum(recv[:, 0], recv[:, 1])
     top = jnp.max(jnp.max(table, axis=0), axis=0, keepdims=True)
     xsend[...] = jnp.broadcast_to(top, (8, 128))
     pl.semaphore_wait(xsem, 2)
     over_x = [
-        remote(xsend, xrecv.at[i], sx.at[i], rx.at[i], to)
+        remote(xsend, xrecv.at[i], sent.at[4], came_x, to)
         for i, to in enumerate(x_peers)
     ]
     for copy in over_x:
         copy.start()
-    for copies in (up, down, over, right, left):
-        for copy in copies.values():
-            copy.wait_send()
-    for copy in back:
-        copy.wait_send()
-    for copy in over_x:
-        copy.wait_recv()
+    left_here(own.at[pl.ds(0, 7)], sent.at[0])
+    left_here(own, sent.at[1])
+    left_here(bank.at[pl.ds(0, 3)], sent.at[2])
+    left_here(res, sent.at[3])
+    landed(xrecv, came_x)
     peak = jnp.maximum(
         jnp.maximum(xsend[...], xrecv[0]), jnp.maximum(xrecv[1], xrecv[2])
     )
     relative = (table - peak[None]).reshape(NZ * 8, 128)
     rel_ref[...] = relative.T[:GROUP, :]
     peak_ref[...] = peak[:1, :]
-    for copy in over_x:
-        copy.wait_send()
+    left_here(xrecv, sent.at[4])
 
 
 def flush(rel_ref, peak_ref, rel_out, peak_out, row, sem):
@@ -312,10 +374,7 @@
             vmem((8, 128), jnp.float32),
             vmem((3, 8, 128), jnp.float32),
             dma((2,)),
-            dma((8,)), dma((8,)), dma((8,)), dma((8,)), dma((8,)), dma((8,)),
-            dma((7,)), dma((7,)), dma((7,)), dma((7,)),
-            dma((15,)), dma((NZ, NC)),
-            dma((3,)), dma((3,)),
+            dma((5,)), dma((8,)), dma((8,)), dma((7,)), dma(()), dma(()),
             pltpu.SemaphoreType.REGULAR,
         ],
         compiler_params=pltpu.CompilerParams(collective_id=0, has_side_effects=True),

time: 42 us -> 40.9 us (0.974)
  Pallas kernels: 41.1 us -> 40 us
    pallas_call x1, Pallas kernels: 40.5 us -> 39.4 us  [per_device(): pl.pallas_call(kernel, out_shape=(vmem((GROUP, NZ * 8), jnp.float32), vme...]
where the time goes in v3:
time: 40.9 us; the launch traced here: 40.8 us
  Pallas kernels  40 us (98%)
  between operations  0.8 us (2%)
    pallas_call x1, Pallas kernels, per_device(): pl.pallas_call(kernel, out_shape=(vmem((GROUP, NZ * 8), jnp.float32), vme...  39.4 us

profile of v3, /device:TPU:1, one launch (start us, length us, event | category | flops | bytes accessed | tf_op | source)
XLA Modules:
  0.0 40.8 jit_solution(9850340634411871589)
XLA Ops:
  0.6 39.4 %shard_map.41 = (f32[64,64]{1,0:T(8,128)S(1)}, f32[1,128]{1,0:T(1,128)S(1)}) custom-call(bf16[64,8,128]{2,1,0:T(8,128)(2,1)} %caps_ref.1, bf16[1024,128]{1,0:T(8,128)(2,1)} %bank_ref.1), custom_call_target="tpu_custom_call" | custom-call | tf_op jit(solution)/shard_map/pallas_call | solution.py:357
  40.0 0.6 %shard_map.42 = (f32[64,64]{1,0:T(8,128)}, f32[64]{0:T(128)}) custom-call(f32[64,64]{1,0:T(8,128)S(1)} %get-tuple-element.4.rel_ref, f32[1,128]{1,0:T(1,128)S(1)} %get-tuple-element.5.peak_ref), custom_call_target="tpu_custom_call" | custom-call | tf_op jit(solution)/shard_map/pallas_call | solution.py:382
